TPU v7x, 128 devices: a whole 4x4x4 slice. The times are simulated.
128 devices in a mesh: band: 32 (over z, y, x_hi), grid: 4 (over x_lo, core).
Axes of the slice: x: 4 (x_hi: 2, x_lo: 2; x = x_hi * 2 + x_lo), y: 4, z: 4, core: 2. Of those that a mesh axis runs over, the one named last changes fastest.
Arguments:
- orbitals: float32 [128, 110592], P('band', 'grid'), may hold values from -6 to 6
Outputs:
- exchange_vectors: float32 [128, 110592], P('band', 'grid')
- margin: float32 [128, 128], P('grid', 'band')
All inputs are finite; a program needn't handle non-finite values.
Results may differ from a plain program's by a relative error of at most 0.00012.
Values sent between devices are 32-bit elements; how exact they have to be, the bound alone decides.
A program may use at most 128 MiB of HBM per device.

v0:
```python
import jax
import jax.numpy as jnp
import numpy as np
from jax import lax
from jax.experimental import pallas as pl
from jax.experimental.pallas import tpu as pltpu
from jax.sharding import PartitionSpec as P

NG = 48
NCELL = 110592
PITCH = 52
SLAB = 216
MESH = pl.DeviceIdType.MESH
F32 = jnp.float32
BF16 = jnp.bfloat16
U1, U2, U3, U5 = 3, 8, 8, 1
VMEM = pl.BlockSpec(memory_space=pltpu.VMEM)


def hartley_rows():
    index = np.arange(NG)
    angles = (index[:, None] * index[None, :] % NG) * (2 * np.pi / NG)
    table = (np.cos(angles) + np.sin(angles)).astype(np.float32)
    high = table.astype(BF16)
    low = (table - high.astype(np.float32)).astype(BF16)
    return jnp.asarray(np.concatenate([high, high, low], axis=1))


def folded(index):
    return ((index + NG // 2) % NG - NG // 2).astype(F32)


def at(b, g):
    return {"band": b, "grid": g}


def slab(g):
    return pl.ds(pl.multiple_of(g * SLAB, 8), SLAB)


def first_tile(m):
    return (27 * m) // 16


def split(value):
    high = value.astype(BF16)
    low = (value - high.astype(F32)).astype(BF16)
    return high, low


def hartley(table, value):
    high, low = split(value)
    stack = jnp.concatenate([high, low, high], axis=0)
    dims = (((1,), (0,)), ((), ()))
    return lax.dot_general(table, stack, dims, preferred_element_type=F32)


def fill_kernel(k_ref):
    lane = lax.broadcasted_iota(jnp.int32, (1, 128), 1)
    y = folded(lax.broadcasted_iota(jnp.int32, (NG, 128), 0))
    x = [folded((l * 128 + lane) % NG) for l in range(3)]
    planes = [y * y + v * v for v in x]

    def plane(z, _):
        depth = z.astype(F32)
        depth = depth * depth
        for l in range(3):
            square = planes[l] + depth
            safe = jnp.where(square > 0, square, 1.0)
            value = (40.0 / NCELL) * (1.0 - jnp.exp(-square / 16.0)) / safe
            value = jnp.where(square > 0, value, 0.0)
            k_ref[l, pl.ds(pl.multiple_of(z * NG, 8), NG), :] = value
        return 0

    lax.fori_loop(0, NG // 2 + 1, plane, 0)

    def mirror(z, _):
        for l in range(3):
            source = pl.ds(pl.multiple_of((NG - z) * NG, 8), NG)
            k_ref[l, pl.ds(pl.multiple_of(z * NG, 8), NG), :] = k_ref[l, source, :]
        return 0

    lax.fori_loop(NG // 2 + 1, NG, mirror, 0)


def exchange_kernel(orb, h_ref, v_out, m_out, a_ref, b_ref, below, o_own, o_oth, k_ref, s_ref, r_ref, va, ob,
                    owed1, sums, owed2, owed3, back1, sumv, back2, vec, vc, part, got, fin,
                    gsend, grecv, osend, orecv, send, recv, vsend, vrecv, psend, precv, fsend, frecv):
    b, g = lax.axis_index("band"), lax.axis_index("grid")
    m, xh, xl, c = b // 2, b % 2, g // 2, g % 2
    far, near = (g + 2) % 4, g + 1 - 2 * c
    across, core = at(b, far), at(b, near)
    up, down = at((b + 1) % 32, far), at((b + 31) % 32, far)
    twin = at(b + 1 - 2 * xh, g)
    mine, theirs = slab(g), slab(far)
    barrier = pltpu.get_barrier_semaphore()
    for peer in (across, core, up, down, at(b, 3 - g), twin):
        pl.semaphore_signal(barrier, inc=1, device_id=peer, device_id_type=MESH)

    def greet(k, _):
        peer = at(2 * ((m + k) % 16) + xh, g)
        pl.semaphore_signal(barrier, inc=1, device_id=peer, device_id_type=MESH)
        return 0

    lax.fori_loop(1, 16, greet, 0)
    for n in range(4):
        a_ref[n, mine, :] = orb[pl.ds(n, SLAB, stride=4), :]
    pl.semaphore_wait(barrier, 21)

    def remote(sends, recvs, sem, src, dst, peer):
        return pltpu.make_async_remote_copy(
            src_ref=src, dst_ref=dst, send_sem=sends.at[sem], recv_sem=recvs.at[sem],
            device_id=peer, device_id_type=MESH,
        )

    def first(sem, src, dst, peer):
        return remote(gsend, grecv, sem, src, dst, peer)

    def copy(sem, src, dst, peer):
        return remote(send, recv, sem, src, dst, peer)

    def own_a(n):
        return a_ref.at[pl.ds(2 * n, 2), mine, :]

    def far_a(n):
        return a_ref.at[pl.ds(2 * n, 2), theirs, :]

    with jax.named_scope("gather_a"):
        a_across = [first(n, own_a(n), own_a(n), across) for n in range(2)]
        a_core = first(2, a_ref.at[:, mine, :], a_ref.at[:, mine, :], core)
        a_far = [first(3 + n, far_a(n), far_a(n), core) for n in range(2)]
        b_up = first(5, a_ref.at[:, mine, :], below, up)
        b_across = first(6, below.at[pl.ds(2 - 2 * xl, 2)], b_ref.at[:, theirs, :], across)
        b_core = first(7, below.at[pl.ds(2 * xl, 2)], b_ref.at[:, theirs, :], core)
        b_far = first(8, b_ref.at[:, mine, :], b_ref.at[:, mine, :], core)
        for started in (a_across[0], a_across[1], b_up, a_core):
            started.start()

        def chunk(n):
            return pl.ds(pl.multiple_of(g * SLAB + 8 * first_tile(n), 8), 16)

        o_own[m] = a_ref[:, chunk(m), :]
        fill_kernel(k_ref)
        for n in range(2):
            a_across[n].wait_recv()
            a_far[n].start()
        b_up.wait_recv()
        b_across.start()
        b_core.start()

        def other(k):
            n = (m + k) % 16
            return remote(osend, orecv, k, a_ref.at[:, chunk(n), :], o_own.at[m], at(2 * n + xh, g))

        def scatter(k, _):
            other(k).start()
            return 0

        lax.fori_loop(1, 16, scatter, 0)
        b_ref[:, theirs, :] = below[pl.ds(2 * xl, 2)]
        a_core.wait_recv()
        a_far[0].wait_recv()
        a_far[1].wait_recv()

    d = 2 * c + xl
    table = h_ref[...]

    def rows(t):
        return pl.ds(t, NG, stride=18)

    def load(ref, i, t):
        return jnp.concatenate([ref[i, rows(t), :], ref[i, rows(t + 1), :]], axis=1)

    def store(ref, j, t, value):
        ref[j, rows(t), :] = value[:, :128]
        ref[j, rows(t + 1), :] = value[:, 128:]

    def forward(f, t, product):
        out = hartley(table, product)
        s_ref[t, f * 48 : (f + 1) * 48, :] = out[:, :128]
        s_ref[t + 1, f * 48 : (f + 1) * 48, :] = out[:, 128:]

    def forward_own(i, _):
        for u in range(U1):
            t = (i * U1 + u) * 2
            single = load(a_ref, d, t)
            for f in range(4):
                forward(4 + f, t, single * load(a_ref, f, t))
        return 0

    def forward_below(i, _):
        for u in range(U1):
            t = (i * U1 + u) * 2
            a0, a1 = load(a_ref, 2 * c, t), load(a_ref, 2 * c + 1, t)
            b0, b1 = load(b_ref, 0, t), load(b_ref, 1, t)
            for f, product in enumerate((a0 * b0, a0 * b1, a1 * b0, a1 * b1)):
                forward(f, t, product)
        return 0

    with jax.named_scope("forward_own"):
        lax.fori_loop(0, 9 // U1, forward_own, 0)
    with jax.named_scope("wait_b"):
        b_across.wait_recv()
        b_far.start()
        b_core.wait_recv()
        b_far.wait_recv()
    with jax.named_scope("forward_below"):
        lax.fori_loop(0, 9 // U1, forward_below, 0)

    def turn_in(i, _):
        for v in range(3):
            for l in range(3):
                block = s_ref[i * 3 + v, l * 128 : (l + 1) * 128, :].T
                for n in range(16):
                    y, z = divmod(v * 128 + n * 8, 48)
                    r_ref[l, pl.ds((i * 8 + y) * PITCH + z, 8), :] = block[n * 8 : (n + 1) * 8, :]
        return 0

    with jax.named_scope("turn_in"):
        lax.fori_loop(0, 6, turn_in, 0)

    def wide(ref, where):
        return jnp.concatenate([ref[0, where, :], ref[1, where, :], ref[2, where, :]], axis=1)

    def keep(where, value):
        for l in range(3):
            r_ref[l, where, :] = value[:, l * 128 : (l + 1) * 128]

    def along_z(i, _):
        for u in range(U2):
            where = pl.ds((i * U2 + u) * PITCH, 48)
            keep(where, hartley(table, wide(r_ref, where)))
        return 0

    def along_y(i, _):
        for u in range(U3):
            z = i * U3 + u
            where = pl.ds(z, 48, stride=PITCH)
            spectrum = hartley(table, wide(r_ref, where))
            keep(where, hartley(table, spectrum * wide(k_ref, pl.ds(z * 48, 48))))
        return 0

    with jax.named_scope("along_z"):
        lax.fori_loop(0, 48 // U2, along_z, 0)
    with jax.named_scope("along_y"):
        lax.fori_loop(0, 48 // U3, along_y, 0)

    with jax.named_scope("o_wait"):

        def gathered(k, _):
            other(k).wait()
            return 0

        lax.fori_loop(1, 16, gathered, 0)
        o_twin = first(9, o_own, o_oth, twin)
        o_twin.start()

    with jax.named_scope("along_z"):
        lax.fori_loop(0, 48 // U2, along_z, 0)

    def turn_out(i, _):
        for v in range(3):
            for l in range(3):
                parts = []
                for n in range(16):
                    y, z = divmod(v * 128 + n * 8, 48)
                    parts.append(r_ref[l, pl.ds((i * 8 + y) * PITCH + z, 8), :])
                s_ref[i * 3 + v, l * 128 : (l + 1) * 128, :] = jnp.concatenate(parts, axis=0).T
        return 0

    with jax.named_scope("turn_out"):
        lax.fori_loop(0, 6, turn_out, 0)

    def potential(f, t):
        span = slice(f * 48, (f + 1) * 48)
        return hartley(table, jnp.concatenate([s_ref[t, span, :], s_ref[t + 1, span, :]], axis=1))

    def backward_x(i, _):
        for u in range(U5):
            t = (i * U5 + u) * 2
            b0, b1 = load(b_ref, 0, t), load(b_ref, 1, t)
            p0, p1 = potential(0, t), potential(1, t)
            a0, a1 = load(a_ref, 2 * c, t), load(a_ref, 2 * c + 1, t)
            store(va, 0, t, -(b0 * p0 + b1 * p1))
            p2, p3 = potential(2, t), potential(3, t)
            store(va, 1, t, -(b0 * p2 + b1 * p3))
            store(ob, 0, t, -(a0 * p0 + a1 * p2))
            store(ob, 1, t, -(a0 * p1 + a1 * p3))
            total = load(va, xl, t)
            for j in range(4):
                total = total - load(a_ref, j, t) * potential(4 + j, t)
            store(va, xl, t, total)
        return 0

    with jax.named_scope("backward_x"):
        lax.fori_loop(0, 9 // U5, backward_x, 0)

    with jax.named_scope("reduce_owed"):
        other_half = pl.ds(pl.multiple_of((1 - xl) * 2 * SLAB, 8), 2 * SLAB)
        own_half = pl.multiple_of(xl * 2 * SLAB, 8)
        a0 = copy(0, va.at[0, other_half, :], back1.at[0], across)
        a1 = copy(1, va.at[1, other_half, :], back1.at[1], across)
        d0 = copy(2, ob.at[:, slab(1 - c), :], owed1.at[0], core)
        d1 = copy(3, ob.at[:, slab(3 - c), :], owed1.at[1], core)
        d0.start()
        d1.start()
        a0.start()
        d0.wait_recv()
        sums[0] = ob[:, slab(c), :] + owed1[0]
        d1.wait_recv()
        sums[1] = ob[:, slab(2 + c), :] + owed1[1]
        x2 = copy(4, sums.at[xl], owed2, across)
        x2.start()
        y0 = copy(5, sums.at[1 - xl], owed3.at[xl], down)
        y0.start()
        a1.start()
        x2.wait_recv()
        y1 = copy(6, owed2, owed3.at[1 - xl], down)
        y1.start()
    with jax.named_scope("reduce_a"):
        a0.wait_recv()
        a1.wait_recv()
        for n in range(2):
            where = pl.ds(pl.multiple_of(own_half + n * SLAB, 8), SLAB)
            sumv[n] = va[:, where, :] + back1[:, n * SLAB : (n + 1) * SLAB, :]
        z0 = copy(7, sumv.at[1 - c], back2, core)
        z0.start()
    with jax.named_scope("reduce_last"):
        y0.wait_recv()
        y1.wait_recv()
        vec[pl.ds(2 * c, 2)] = sumv[c] + owed3[c]
        z0.wait_recv()
        vec[pl.ds(2 - 2 * c, 2)] = back2[...] + owed3[1 - c]

    def piece_of(n):
        return pl.ds(pl.multiple_of(8 * first_tile(n), 8), 16)

    def spread(k):
        n = (m + k) % 16
        return remote(vsend, vrecv, k, vec.at[:, piece_of(n), :], vc.at[m], at(2 * n + xh, g))

    def spread_start(k, _):
        spread(k).start()
        return 0

    with jax.named_scope("spread_v"):
        lax.fori_loop(1, 16, spread_start, 0)
        vc[m] = vec[:, piece_of(m), :]
        for n in range(4):
            v_out[pl.ds(n, SLAB, stride=4), :] = vec[n]
        for sent in (*a_across, a_core, *a_far, b_up, b_across, b_core, b_far, a0, a1, d0, d1, x2, y0, y1, z0):
            sent.wait_send()
        o_twin.wait()

        def spread_wait(k, _):
            spread(k).wait()
            return 0

        lax.fori_loop(1, 16, spread_wait, 0)

    double = (first_tile(m + 1) - first_tile(m) - 1).astype(F32)
    dims = (((1,), (1,)), ((), ()))

    def products(r, total):
        both = []
        for n in range(16):
            own, oth = o_own[n, :, r, :], o_oth[n, :, r, :]
            both += [jnp.where(xh == 0, own, oth), jnp.where(xh == 0, oth, own)]
        some = jnp.concatenate([vc[n, :, r, :] for n in range(16)], axis=0)
        if r >= 8:
            some = some * double
        oh, ol = split(jnp.concatenate(both, axis=0))
        vh, vl = split(some)
        left = jnp.concatenate([vh, vl, vh], axis=1)
        right = jnp.concatenate([oh, oh, ol], axis=1)
        return total + lax.dot_general(left, right, dims, preferred_element_type=F32)

    with jax.named_scope("products"):
        total = jnp.zeros((64, 128), F32)
        for r in range(16):
            total = products(r, total)
        part[...] = (total * (1.0 / NCELL)).reshape(8, 8, 128)

    def piece(k):
        n = (m + k) % 16
        return remote(psend, precv, k, part.at[n // 2], got.at[k], at(2 * n + xh, g))

    def deal(k, _):
        piece(k).start()
        return 0

    def dealt(k, acc):
        piece(k).wait()
        return acc + got[k]

    with jax.named_scope("deal"):
        lax.fori_loop(1, 16, deal, 0)
        fin[0] = lax.fori_loop(1, 16, dealt, part[m // 2])
    with jax.named_scope("last"):
        last = [remote(fsend, frecv, k, fin.at[0], fin.at[k], at(b, (g + k) % 4)) for k in range(1, 4)]
        for sent in last:
            sent.start()
        for sent in last:
            sent.wait()
        whole = fin[0] + fin[1] + fin[2] + fin[3]
        quarter = jnp.where(m % 2 == 0, whole[:4], whole[4:])
        low = jnp.where(g % 2 == 0, quarter[:, :32], quarter[:, 32:64])
        high = jnp.where(g % 2 == 0, quarter[:, 64:96], quarter[:, 96:])
        m_out[...] = jnp.where(g < 2, low, high)


def on_device(orbitals):
    shape = jax.ShapeDtypeStruct
    dma = pltpu.SemaphoreType.DMA

    def room(*dims):
        return pltpu.VMEM(dims, F32)

    packed = orbitals.reshape(4, SLAB, 128).transpose(1, 0, 2).reshape(4 * SLAB, 128)
    half = room(2, 2, SLAB, 128)
    vectors, margin = pl.pallas_call(
        exchange_kernel,
        out_shape=(shape((4 * SLAB, 128), F32), shape((4, 32), F32)),
        in_specs=[VMEM] * 2,
        out_specs=(VMEM, VMEM),
        scratch_shapes=[
            room(4, 864, 128), room(2, 864, 128), room(4, SLAB, 128),
            room(16, 4, 16, 128), room(16, 4, 16, 128), room(3, NG * NG, 128),
            room(18, 384, 128), room(3, NG * PITCH, 128), room(2, 864, 128), room(2, 864, 128),
            half, half, room(2, SLAB, 128), half, room(2, 2 * SLAB, 128), half,
            room(2, SLAB, 128), room(4, SLAB, 128), room(16, 4, 16, 128), room(8, 8, 128),
            room(16, 8, 128), room(4, 8, 128),
            dma((10,)), dma((10,)), dma((16,)), dma((16,)), dma((8,)), dma((8,)),
            dma((16,)), dma((16,)), dma((16,)), dma((16,)), dma((4,)), dma((4,)),
        ],
        compiler_params=pltpu.CompilerParams(
            collective_id=0, has_side_effects=True, vmem_limit_bytes=50 * 1024 * 1024
        ),
        name="exchange",
    )(packed, hartley_rows())
    vectors = vectors.reshape(SLAB, 4, 128).transpose(1, 0, 2).reshape(4, SLAB * 128)
    return vectors, margin.T


def solution(mesh):
    return jax.shard_map(
        on_device,
        mesh=mesh,
        in_specs=(P("band", "grid"),),
        out_specs=(P("band", "grid"), P("grid", "band")),
        check_vma=False,
    )
```

profile of v0, /device:TPU:1, one launch (start us, length us, event | category | flops | bytes accessed | tf_op | source)
XLA Modules:
  0.0 91.6 jit_solution(4850874102307154141)
XLA Ops:
  0.6 0.0 copy-start
  0.6 1.0 %copy-done = f32[4,27648]{1,0:T(4,128)S(1)} copy-done((f32[4,27648]{1,0:T(4,128)S(1)}, f32[4,27648]{1,0:T(4,128)}, u32[]{:S(2)}) %copy-start) | copy-done | bytes 442392
  1.6 0.0 copy-start.1
  1.6 0.7 copy-done.1
  2.4 87.8 %exchange.1 = (f32[864,128]{1,0:T(8,128)S(1)}, f32[4,32]{1,0:T(4,128)S(1)}) custom-call(f32[864,128]{1,0:T(8,128)S(1)} %bitcast.11, bf16[48,144]{1,0:T(8,128)(2,1)S(1)} %copy-done.1), custom_call_target="tpu_custom_call" | custom-call | tf_op jit(solution)/shard_map/exchange/pallas_call | solution.py:421
  90.2 0.8 copy.8
  91.0 0.6 copy.9
Async XLA Ops:
  0.6 1.0 %copy-start = (f32[4,27648]{1,0:T(4,128)S(1)}, f32[4,27648]{1,0:T(4,128)}, u32[]{:S(2)}) copy-start(f32[4,27648]{1,0:T(4,128)} %param.2) | copy-start | bytes 1327108
  1.6 0.7 copy-start.1
where the time goes:
time: 92.2 us; the launch traced here: 91.6 us
  Pallas kernels  87.8 us (95%)
  local copies, waits for them, and re-layouts  3.09 us (3%)
    pallas_call x1, Pallas kernels, on_device(): pl.pallas_call(exchange_kernel, out_shape=(shape((4 * SLAB, 128), F32), s...  87.8 us
    unnamed x6, local copies, waits for them, and re-layouts  3.09 us

commit v1 on v0

v1 whole, which is shorter than its diff:
```python
import jax
import jax.numpy as jnp
import numpy as np
from jax import lax
from jax.experimental import pallas as pl
from jax.experimental.pallas import tpu as pltpu
from jax.sharding import PartitionSpec as P

NG = 48
NCELL = 110592
PITCH = 52
SLAB = 216
MESH = pl.DeviceIdType.MESH
F32 = jnp.float32
BF16 = jnp.bfloat16
U1, U2, U3, U5 = 3, 8, 8, 1
VMEM = pl.BlockSpec(memory_space=pltpu.VMEM)


def hartley_rows():
    index = np.arange(NG)
    angles = (index[:, None] * index[None, :] % NG) * (2 * np.pi / NG)
    table = (np.cos(angles) + np.sin(angles)).astype(np.float32)
    high = table.astype(BF16)
    low = (table - high.astype(np.float32)).astype(BF16)
    return jnp.asarray(np.concatenate([high, high, low], axis=1))


def folded(index):
    return ((index + NG // 2) % NG - NG // 2).astype(F32)


def at(b, g):
    return {"band": b, "grid": g}


def slab(g):
    return pl.ds(pl.multiple_of(g * SLAB, 8), SLAB)


def first_tile(m):
    return (27 * m) // 16


def split(value):
    high = value.astype(BF16)
    low = (value - high.astype(F32)).astype(BF16)
    return high, low


def hartley(table, value):
    high, low = split(value)
    stack = jnp.concatenate([high, low, high], axis=0)
    dims = (((1,), (0,)), ((), ()))
    return lax.dot_general(table, stack, dims, preferred_element_type=F32)


def fill_kernel(k_ref):
    lane = lax.broadcasted_iota(jnp.int32, (1, 128), 1)
    y = folded(lax.broadcasted_iota(jnp.int32, (NG, 128), 0))
    x = [folded((l * 128 + lane) % NG) for l in range(3)]
    planes = [y * y + v * v for v in x]

    def plane(z, _):
        depth = z.astype(F32)
        depth = depth * depth
        for l in range(3):
            square = planes[l] + depth
            safe = jnp.where(square > 0, square, 1.0)
            value = (40.0 / NCELL) * (1.0 - jnp.exp(-square / 16.0)) / safe
            value = jnp.where(square > 0, value, 0.0)
            k_ref[l, pl.ds(pl.multiple_of(z * NG, 8), NG), :] = value
        return 0

    lax.fori_loop(0, NG // 2 + 1, plane, 0)

    def mirror(z, _):
        for l in range(3):
            source = pl.ds(pl.multiple_of((NG - z) * NG, 8), NG)
            k_ref[l, pl.ds(pl.multiple_of(z * NG, 8), NG), :] = k_ref[l, source, :]
        return 0

    lax.fori_loop(NG // 2 + 1, NG, mirror, 0)


def exchange_kernel(orb_hbm, h_hbm, v_out, m_out, orb, h_ref, load_sem, a_ref, b_ref, o_all, k_ref, s_ref, r_ref, q_ref,
                    va, ob, owed1, sums, owed3, back1, back2, back3, vec, vc, part, near_part, rows_out, rows_in,
                    gsend, grecv, osend, orecv, send, recv, vsend, vrecv, psend, precv, nsend, nrecv):
    b, g = lax.axis_index("band"), lax.axis_index("grid")
    m, xh, xl, c = b // 2, b % 2, g // 2, g % 2
    far, near = (g + 2) % 4, g + 1 - 2 * c
    across, core, diagonal = at(b, far), at(b, near), at(b, 3 - g)
    up, up_far = at((b + 1) % 32, g), at((b + 1) % 32, far)
    down, down_far = at((b + 31) % 32, g), at((b + 31) % 32, far)
    twin = at(b + 1 - 2 * xh, g)
    mine, theirs = slab(g), slab(far)
    fetch = pltpu.make_async_copy(orb_hbm, orb, load_sem.at[0])
    fetch.start()
    fetch_table = pltpu.make_async_copy(h_hbm, h_ref, load_sem.at[1])
    fetch_table.start()
    barrier = pltpu.get_barrier_semaphore()
    for peer in (up, up_far, down, down_far):
        pl.semaphore_signal(barrier, inc=1, device_id=peer, device_id_type=MESH)

    for peer in (across, core, diagonal):
        pl.semaphore_signal(barrier, inc=1, device_id=peer, device_id_type=MESH)

    def greet(k, _):
        peer = at(2 * ((m + k) % 16) + xh, g)
        pl.semaphore_signal(barrier, inc=1, device_id=peer, device_id_type=MESH)
        return 0

    lax.fori_loop(1, 16, greet, 0)
    fetch.wait()
    for n in range(4):
        a_ref[n, mine, :] = orb[pl.ds(n, SLAB, stride=4), :]
    pl.semaphore_wait(barrier, 22)

    def remote(sends, recvs, sem, src, dst, peer, recv_at=None):
        return pltpu.make_async_remote_copy(
            src_ref=src, dst_ref=dst, send_sem=sends.at[sem], recv_sem=recvs.at[sem if recv_at is None else recv_at],
            device_id=peer, device_id_type=MESH,
        )

    def first(sem, src, dst, peer):
        return remote(gsend, grecv, sem, src, dst, peer)

    def copy(sem, src, dst, peer):
        return remote(send, recv, sem, src, dst, peer)

    def own_a(n):
        return a_ref.at[pl.ds(2 * n, 2), mine, :]

    def far_a(n):
        return a_ref.at[pl.ds(2 * n, 2), theirs, :]

    with jax.named_scope("gather_a"):
        a_across = [first(n, own_a(n), own_a(n), across) for n in range(2)]
        a_core = first(2, a_ref.at[:, mine, :], a_ref.at[:, mine, :], core)
        a_far = [first(3 + n, far_a(n), far_a(n), core) for n in range(2)]
        b_near = first(5, a_ref.at[pl.ds(2 - 2 * xl, 2), mine, :], b_ref.at[:, mine, :], up_far)
        b_wide = first(6, a_ref.at[pl.ds(2 * xl, 2), mine, :], b_ref.at[:, mine, :], up)
        b_core = first(7, b_ref.at[:, theirs, :], b_ref.at[:, theirs, :], core)
        b_far = first(8, b_ref.at[:, mine, :], b_ref.at[:, mine, :], core)
        for started in (a_across[0], b_wide, a_across[1], b_near, a_core):
            started.start()

        def chunk(n):
            return pl.ds(pl.multiple_of(g * SLAB + 8 * first_tile(n), 8), 16)

        def other(k):
            n = (m + k) % 16
            return remote(osend, orecv, k, a_ref.at[:, chunk(n), :], o_all.at[m, xh], at(2 * n + xh, g))

        def scatter(k, _):
            other(k).start()
            return 0

        lax.fori_loop(1, 16, scatter, 0)
        o_all[m, xh] = a_ref[:, chunk(m), :]
        fill_kernel(k_ref)
        a_across[0].wait_recv()
        a_far[0].start()
        b_near.wait_recv()
        b_core.start()
        a_across[1].wait_recv()
        a_far[1].start()
        a_core.wait_recv()
        a_far[0].wait_recv()
        a_far[1].wait_recv()

    d = 2 * c + xl
    fetch_table.wait()
    table = h_ref[...]

    def rows(t):
        return pl.ds(t, NG, stride=18)

    def load(ref, i, t):
        return jnp.concatenate([ref[i, rows(t), :], ref[i, rows(t + 1), :]], axis=1)

    def store(ref, j, t, value):
        ref[j, rows(t), :] = value[:, :128]
        ref[j, rows(t + 1), :] = value[:, 128:]

    def forward(f, t, product):
        out = hartley(table, product)
        s_ref[t, f * 48 : (f + 1) * 48, :] = out[:, :128]
        s_ref[t + 1, f * 48 : (f + 1) * 48, :] = out[:, 128:]

    def forward_own(i, _):
        for u in range(U1):
            t = (i * U1 + u) * 2
            single = load(a_ref, d, t)
            for f in range(4):
                forward(4 + f, t, single * load(a_ref, f, t))
        return 0

    def forward_below(i, _):
        for u in range(U1):
            t = (i * U1 + u) * 2
            a0, a1 = load(a_ref, 2 * c, t), load(a_ref, 2 * c + 1, t)
            b0, b1 = load(b_ref, 0, t), load(b_ref, 1, t)
            for f, product in enumerate((a0 * b0, a0 * b1, a1 * b0, a1 * b1)):
                forward(f, t, product)
        return 0

    with jax.named_scope("forward_own"):
        lax.fori_loop(0, 9 // U1, forward_own, 0)
    with jax.named_scope("wait_b"):
        b_wide.wait_recv()
        b_far.start()

        b_core.wait_recv()
        b_far.wait_recv()
    with jax.named_scope("o_wait"):

        def gathered(k, _):
            other(k).wait()
            return 0

        lax.fori_loop(1, 16, gathered, 0)
        o_twin = first(9, o_all.at[:, xh], o_all.at[:, xh], twin)
        o_twin.start()

    with jax.named_scope("forward_below"):
        lax.fori_loop(0, 9 // U1, forward_below, 0)

    def turn_in(i, _):
        for v in range(3):
            for l in range(3):
                block = s_ref[i * 3 + v, l * 128 : (l + 1) * 128, :].T
                for n in range(16):
                    y, z = divmod(v * 128 + n * 8, 48)
                    r_ref[l, pl.ds((i * 8 + y) * PITCH + z, 8), :] = block[n * 8 : (n + 1) * 8, :]
        return 0

    with jax.named_scope("turn_in"):
        lax.fori_loop(0, 6, turn_in, 0)

    def passes(source, target, where, count, scale=None):
        tiles = [(u, l) for u in range(count) for l in range(3)]
        for p in range(0, len(tiles), 2):
            pair = tiles[p : p + 2]
            value = jnp.concatenate([source[l, where(u), :] for u, l in pair], axis=1)
            out = hartley(table, value)
            for j, (u, l) in enumerate(pair):
                piece = out[:, 128 * j : 128 * (j + 1)]
                if scale is not None:
                    piece = piece * k_ref[l, scale(u), :]
                target[l, where(u), :] = piece

    def along_z(source, target):
        def step(i, _):
            passes(source, target, lambda u: pl.ds((i * U2 + u) * PITCH, 48), U2)
            return 0

        lax.fori_loop(0, 48 // U2, step, 0)

    def along_y(source, target, scaled):
        def step(i, _):
            passes(source, target, lambda u: pl.ds(i * U3 + u, 48, stride=PITCH), U3,
                   (lambda u: pl.ds(pl.multiple_of((i * U3 + u) * 48, 8), 48)) if scaled else None)
            return 0

        lax.fori_loop(0, 48 // U3, step, 0)

    with jax.named_scope("along_z"):
        along_z(r_ref, q_ref)
    with jax.named_scope("along_y"):
        along_y(q_ref, r_ref, True)
    with jax.named_scope("along_y"):
        along_y(r_ref, q_ref, False)
    with jax.named_scope("along_z"):
        along_z(q_ref, r_ref)

    def turn_out(i, _):
        for v in range(3):
            for l in range(3):
                parts = []
                for n in range(16):
                    y, z = divmod(v * 128 + n * 8, 48)
                    parts.append(r_ref[l, pl.ds((i * 8 + y) * PITCH + z, 8), :])
                s_ref[i * 3 + v, l * 128 : (l + 1) * 128, :] = jnp.concatenate(parts, axis=0).T
        return 0

    with jax.named_scope("turn_out"):
        lax.fori_loop(0, 6, turn_out, 0)

    def potential(f, t):
        span = slice(f * 48, (f + 1) * 48)
        return hartley(table, jnp.concatenate([s_ref[t, span, :], s_ref[t + 1, span, :]], axis=1))

    def backward_below(i, _):
        for u in range(U5):
            t = (i * U5 + u) * 2
            b0, b1 = load(b_ref, 0, t), load(b_ref, 1, t)
            p0, p1 = potential(0, t), potential(1, t)
            a0, a1 = load(a_ref, 2 * c, t), load(a_ref, 2 * c + 1, t)
            store(va, 0, t, -(b0 * p0 + b1 * p1))
            p2, p3 = potential(2, t), potential(3, t)
            store(va, 1, t, -(b0 * p2 + b1 * p3))
            store(ob, 0, t, -(a0 * p0 + a1 * p2))
            store(ob, 1, t, -(a0 * p1 + a1 * p3))
        return 0

    def backward_own(i, _):
        for u in range(U5):
            t = (i * U5 + u) * 2
            total = load(va, xl, t)
            for j in range(4):
                total = total - load(a_ref, j, t) * potential(4 + j, t)
            store(va, xl, t, total)
        return 0

    def to_far(e):
        return remote(send, recv, e, va.at[e, theirs, :], back1.at[e], across)

    def to_core(e):
        return remote(send, recv, 2 + e, va.at[e, slab(near), :], back2.at[e], core)

    def to_diagonal(e):
        return remote(send, recv, 4 + e, va.at[e, slab(3 - g), :], back3.at[e], diagonal)

    def owed(j):
        return remote(send, recv, 6 + j, sums.at[j], owed3.at[xl], at((b + 31) % 32, 2 * j + c), 6 + xl)

    def hand_out(e):
        to_far(e).start()
        to_diagonal(e).start()
        to_core(e).start()

    def twofold(n):
        return first_tile(n + 1) - first_tile(n) == 2

    def spread(k, e, rows):
        n = (m + k) % 16
        source = vec.at[e, :, pl.ds(pl.multiple_of(8 * first_tile(n), 8), rows), :]
        target = vc.at[m, e, :, pl.ds(0, rows), :]
        return remote(vsend, vrecv, 16 * e + k, source, target, at(2 * n + xh, g))

    def either(flag, act):
        @pl.when(flag)
        def _():
            act(16)

        @pl.when(jnp.logical_not(flag))
        def _():
            act(8)

    def collect(e):
        for copy_of in (to_far, to_core, to_diagonal):
            copy_of(e).wait_recv()
        vec[e, c] = va[e, mine, :] + back1[e] + owed3[c, e]
        vec[e, 1 - c] = back2[e] + back3[e] + owed3[1 - c, e]

        def start(k, _):
            either(twofold((m + k) % 16), lambda rows: spread(k, e, rows).start())
            return 0

        lax.fori_loop(1, 16, start, 0)
        vc[m, e] = vec[e, :, pl.ds(pl.multiple_of(8 * first_tile(m), 8), 16), :]

    def spread_wait(e):
        def wait(k, _):
            either(twofold((m + k) % 16), lambda rows: spread(k, e, rows).wait_send())
            either(twofold(m), lambda rows: spread(k, e, rows).wait_recv())
            return 0

        lax.fori_loop(1, 16, wait, 0)

    with jax.named_scope("backward_below"):
        lax.fori_loop(0, 9 // U5, backward_below, 0)
        d0 = copy(8, ob.at[:, slab(1 - c), :], owed1.at[0], core)
        d1 = copy(9, ob.at[:, slab(3 - c), :], owed1.at[1], core)
        d0.start()
        d1.start()
        hand_out(1 - xl)
    with jax.named_scope("backward_own"):
        lax.fori_loop(0, 9 // U5, backward_own, 0)
    with jax.named_scope("reduce_owed"):
        d0.wait_recv()
        sums[0] = ob[:, slab(c), :] + owed1[0]
        owed(0).start()
        d1.wait_recv()
        sums[1] = ob[:, slab(2 + c), :] + owed1[1]
        owed(1).start()
        hand_out(xl)
        for sent in (*a_across, a_core, *a_far, b_near, b_wide, b_core, b_far):
            sent.wait_send()
        for j in range(2):
            remote(send, recv, 6 + j, sums.at[j], owed3.at[j], down, 6 + j).wait_recv()
    with jax.named_scope("collect_first"):
        collect(xl)
    with jax.named_scope("collect_last"):
        collect(1 - xl)
    with jax.named_scope("spread_first"):
        for e in range(2):
            for n in range(2):
                v_out[pl.ds(2 * n + e, SLAB, stride=4), :] = vec[e, n]
        for e in range(2):
            for copy_of in (to_far, to_core, to_diagonal):
                copy_of(e).wait_send()
        for sent in (d0, d1, owed(0), owed(1)):
            sent.wait_send()
        o_twin.wait_send()
        first(9, o_all.at[:, xh], o_all.at[:, 1 - xh], twin).wait_recv()
        spread_wait(xl)
    with jax.named_scope("spread_last"):
        spread_wait(1 - xl)

    with jax.named_scope("products"):
        dims = (((1,), (1,)), ((), ()))
        o_rows, v_rows = o_all.reshape(2048, 128), vc.reshape(1024, 128)
        total = jnp.zeros((64, 128), F32)
        for r in range(16):
            some = v_rows[pl.ds(r, 64, stride=16), :]
            if r >= 8:
                some = jnp.where(twofold(m), some, 0.0)
            oh, ol = split(o_rows[pl.ds(r, 128, stride=16), :])
            vh, vl = split(some)
            left = jnp.concatenate([vh, vl, vh], axis=1)
            right = jnp.concatenate([oh, oh, ol], axis=1)
            total = total + lax.dot_general(left, right, dims, preferred_element_type=F32)
        total = total * (1.0 / NCELL)
        lane = lax.broadcasted_iota(jnp.int32, (16, 128), 1) // 32
        slots = (0, 2, 1, 3)
        kinds = [jnp.concatenate([total[4 * n + k : 4 * n + k + 1] for n in range(16)], axis=0) for k in slots]
        for q in range(4):
            row = kinds[q]
            for k in range(4):
                if k != q:
                    row = jnp.where(lane == k, pltpu.roll(kinds[k], 32 * ((k - q) % 4), 1), row)
            part[q] = row

    with jax.named_scope("deal_group"):
        others = [
            remote(nsend, nrecv, k, part.at[(g + k) % 4], near_part.at[k], at(b, (g + k) % 4)) for k in range(1, 4)
        ]
        for sent in others:
            sent.start()
        for sent in others:
            sent.wait()
        group_sum = part[g] + near_part[1] + near_part[2] + near_part[3]
        for n in range(16):
            rows_out[n] = group_sum[n : n + 1, :]

    def deal(k):
        n = (m + k) % 16
        return remote(psend, precv, k, rows_out.at[n], rows_in.at[k], at(2 * n + xh, g))

    def deal_start(k, _):
        deal(k).start()
        return 0

    def deal_wait(k, total):
        deal(k).wait()
        return total + rows_in[k]

    with jax.named_scope("deal"):
        lax.fori_loop(1, 16, deal_start, 0)
        whole = lax.fori_loop(1, 16, deal_wait, rows_out[m])
        for k in range(4):
            m_out[k : k + 1, :] = whole[:, 32 * k : 32 * (k + 1)]


def on_device(orbitals):
    shape = jax.ShapeDtypeStruct
    dma = pltpu.SemaphoreType.DMA

    def room(*dims):
        return pltpu.VMEM(dims, F32)

    packed = orbitals.reshape(4, SLAB, 128).transpose(1, 0, 2).reshape(4 * SLAB, 128)
    half = room(2, 2, SLAB, 128)
    vectors, margin = pl.pallas_call(
        exchange_kernel,
        out_shape=(shape((4 * SLAB, 128), F32), shape((4, 32), F32)),
        in_specs=[pl.BlockSpec(memory_space=pltpu.HBM)] * 2,
        out_specs=(VMEM, VMEM),
        scratch_shapes=[
            room(4 * SLAB, 128), pltpu.VMEM((NG, 3 * NG), BF16), dma((2,)), room(4, 864, 128), room(2, 864, 128),
            room(16, 2, 4, 16, 128), room(3, NG * NG, 128), room(18, 384, 128), room(3, NG * PITCH, 128),
            room(3, NG * PITCH, 128), room(2, 864, 128), room(2, 864, 128), half, half, half,
            room(2, SLAB, 128), room(2, SLAB, 128), room(2, SLAB, 128), half, room(16, 2, 2, 16, 128),
            room(4, 16, 128), room(4, 16, 128), room(16, 1, 128), room(16, 1, 128),
            dma((10,)), dma((10,)), dma((16,)), dma((16,)), dma((10,)), dma((10,)),
            dma((32,)), dma((32,)), dma((16,)), dma((16,)), dma((4,)), dma((4,)),
        ],
        compiler_params=pltpu.CompilerParams(
            collective_id=0, has_side_effects=True, vmem_limit_bytes=67043328
        ),
        name="exchange",
    )(packed, hartley_rows())
    vectors = vectors.reshape(SLAB, 4, 128).transpose(1, 0, 2).reshape(4, SLAB * 128)
    return vectors, margin.T


def solution(mesh):
    return jax.shard_map(
        on_device,
        mesh=mesh,
        in_specs=(P("band", "grid"),),
        out_specs=(P("band", "grid"), P("grid", "band")),
        check_vma=False,
    )
```

time: 92.2 us -> 75.1 us (0.81)
  Pallas kernels: 87.8 us -> 71.2 us
    pallas_call x1, Pallas kernels: 87.8 us -> 71.2 us  [on_device(): pl.pallas_call(exchange_kernel, out_shape=(shape((4 * SLAB, 128), F32), s...]
    unnamed x6 -> x4, local copies, waits for them, and re-layouts: 3.09 us -> 2.39 us
where the time goes in v1:
time: 75.1 us; the launch traced here: 74.2 us
  Pallas kernels  71.2 us (95%)
  local copies, waits for them, and re-layouts  2.39 us (3%)
    pallas_call x1, Pallas kernels, on_device(): pl.pallas_call(exchange_kernel, out_shape=(shape((4 * SLAB, 128), F32), s...  71.2 us
    unnamed x4, local copies, waits for them, and re-layouts  2.39 us

profile of v1, /device:TPU:1, one launch (start us, length us, event | category | flops | bytes accessed | tf_op | source)
XLA Modules:
  0.0 74.2 jit_solution(3578095781980243661)
XLA Ops:
  0.6 71.2 %exchange.1 = (f32[864,128]{1,0:T(8,128)}, f32[4,32]{1,0:T(4,128)}) custom-call(f32[864,128]{1,0:T(8,128)} %bitcast.11, bf16[48,144]{1,0:T(8,128)(2,1)} %constant.2.clone.h_hbm), custom_call_target="tpu_custom_call" | custom-call | tf_op jit(solution)/shard_map/exchange/pallas_call | solution.py:476
  71.8 0.0 copy-start
  71.8 1.8 %copy.8 = f32[4,27648]{1,0:T(4,128)} copy(f32[4,27648]{1,0:T(4,128)} %bitcast.12) | data formatting | bytes 884736
  73.6 0.0 copy-done
  73.6 0.6 copy.9
Async XLA Ops:
  71.8 1.8 %copy-start = (f32[4,32]{1,0:T(4,128)S(1)}, f32[4,32]{1,0:T(4,128)}, u32[]{:S(2)}) copy-start(f32[4,32]{1,0:T(4,128)} %get-tuple-element.5) | copy-start | bytes 1540
